TPU v7x, 256 devices: a whole 4x4x8 slice. The times are simulated.
256 devices in a mesh: seq: 64 (over z, y, core), comp: 4 (over x).
Axes of the slice: x: 4, y: 4, z: 8, core: 2. Of those that a mesh axis runs over, the one named last changes fastest.
Arguments:
- points: float32 [131072, 256], P('seq'), may hold values from -6 to 6
- assign: int32 [64, 2048], P('seq'), may hold values from 0 to 3, never falling along the last dimension, each value on 1 to 1024 neighbouring positions
- plan: int32 [64, 4], P('seq'), may hold values from 64 to 255
- init_mass: float32 [1024], P('comp'), may hold values from 0.00024414062 to 0.00390625
- init_means: float32 [1024, 256], P('comp'), may hold values from -3 to 3
- init_vars: float32 [1024, 256], P('comp'), may hold values from 0.5 to 2
Outputs:
- dev_logmass: float32 [64, 1024], P('seq', 'comp')
- dev_means: float32 [64, 1024, 256], P('seq', 'comp')
- dev_vars: float32 [64, 1024, 256], P('seq', 'comp')
- final_logmass: float32 [64, 1024], P('seq', 'comp')
- final_means: float32 [64, 1024, 256], P('seq', 'comp')
- final_vars: float32 [64, 1024, 256], P('seq', 'comp')
Inputs may be any that keep to these rules, and one draw needn't show every extreme that they name: `assign`: in each row, minibatch numbers never fall along the row and every minibatch has at least one point.
All inputs are finite; a program needn't handle non-finite values.
Results may differ from a plain program's by a relative error of at most 0.0003.
Values sent between devices are 32-bit elements; how exact they have to be, the bound alone decides.
A program may use at most 64 MiB of HBM per device.

v0:
```python
import jax
import jax.numpy as jnp
from jax import lax
from jax.sharding import Mesh
from jax.sharding import PartitionSpec as P

SEQ = ("seq_0", "seq_1", "seq_2")


VAR_PRIOR = 0.01
best_precision = lax.Precision.HIGHEST


def copy_for_each(x, axis):
    length = lax.axis_size(axis)
    return lax.all_to_all(jnp.broadcast_to(x[None], (length, *x.shape)), axis, 0, 0, tiled=True)


def all_in_one(x, axis):
    leaves = jax.tree.leaves(x)
    sequence = sorted(range(len(leaves)), key=lambda k: -leaves[k].size)
    width = (1, *leaves[sequence[0]].shape)[-1]
    lines = [
        jnp.pad(leaves[k].reshape(-1), (0, -leaves[k].size % width)).reshape(-1, width)
        for k in sequence
    ]
    both, at, found = (copy_for_each(jnp.concatenate(lines), axis), 0, {})
    for k, line in zip(sequence, lines):
        share = both[:, at : at + len(line)].reshape(len(both), -1)
        found[k] = share[:, : leaves[k].size].reshape(-1, *leaves[k].shape)
        at += len(line)
    numbers = iter(range(len(leaves)))
    return jax.tree.map(lambda _: found[next(numbers)], x)


def folded_in_pairs(pieces, combine):
    while len(jax.tree.leaves(pieces)[0]) > 1:
        pieces = jax.vmap(combine)(
            *(jax.tree.map(lambda part: part[side::2], pieces) for side in (0, 1))
        )
    return jax.tree.map(lambda part: part[0], pieces)


def merged(x, axis, combine):
    pieces = all_in_one(x, axis)
    return folded_in_pairs(pieces, combine)


def neutral_like(x, identity):
    return jax.tree.map(
        lambda a, e: jnp.broadcast_to(jnp.asarray(e, a.dtype), a.shape), x, identity
    )


def carried_in(x, axes, combine, identity):
    before = start = neutral_like(x, identity)
    so_far = x
    for axis in reversed(axes):
        length, here = (lax.axis_size(axis), lax.axis_index(axis))
        pieces = jax.tree.map(lambda part: lax.all_gather(part, axis), so_far)
        inside, so_far = (start, start)
        for k in range(length):
            passed = k < here
            so_far = combine(so_far, jax.tree.map(lambda part: part[k], pieces))
            inside = jax.tree.map(lambda new, old: jnp.where(passed, new, old), so_far, inside)
        before = combine(inside, before)
    return before


def carried_in_2(x, axis, combine, identity):
    length, here = (lax.axis_size(axis), lax.axis_index(axis))
    passed = jnp.arange(length) > here

    def kept(part, zero, own):
        part = jnp.where(
            passed.reshape(-1, *(1 for _ in own.shape)), part, jnp.asarray(zero, own.dtype)
        )
        return part[::-1]

    pieces = copy_for_each(x, axis)
    return folded_in_pairs(kept(pieces, identity, x), combine)


def in_blocks(x, dim, length):
    shape = x.shape
    tiles = x.reshape(*shape[:dim], length, shape[dim] // length, *shape[dim + 1 :])
    return jnp.moveaxis(tiles, dim, 0)


def sum_at_owner(x, axis, dim):
    tiles = in_blocks(x, dim, lax.axis_size(axis))
    arrived = lax.all_to_all(tiles, axis, split_axis=0, concat_axis=0, tiled=True)
    return arrived.sum(axis=0)


def sum_by_axis(x, axes, dim):
    far, near = axes
    own = sum_at_owner(in_blocks(x, dim, lax.axis_size(far)), near, dim + 1)
    return jnp.sum(lax.all_to_all(own, far, 0, 0, tiled=True), axis=0)


def filled_up(lines, length):
    spare = -lines.shape[0] % length
    if not spare:
        return lines
    return jnp.concatenate([lines, jnp.zeros((spare, *lines.shape[1:]), lines.dtype)])


def laid_out(tiles, dim):
    tiles = jnp.moveaxis(tiles, 0, dim)
    shape = tiles.shape
    return tiles.reshape(*shape[:dim], shape[dim] * shape[dim + 1], *shape[dim + 2 :])


def gather_axes(x, axes, dim):
    far, near = axes
    first = copy_for_each(x, far)
    tiles = jnp.swapaxes(copy_for_each(first, near), 0, 1)
    return laid_out(tiles.reshape(-1, *x.shape), dim)


def total_of(x, axes):
    own = sum_by_axis(filled_up(x, lax.axis_size(axes[0]) * lax.axis_size(axes[1])), axes, 0)
    whole = gather_axes(own, axes, 0)
    return whole[: len(x)].reshape(x.shape)


def together(arrays, axis):
    ravelled, at, finished = (jnp.concatenate([a.reshape(-1) for a in arrays]), 0, [])
    so_far = total_of(ravelled, axis)
    for a in arrays:
        finished.append(so_far[at : at + a.size].reshape(a.shape))
        at += a.size
    return tuple(finished)


def prepare(init_mass, init_means, init_vars):
    inverse = 1.0 / init_vars
    lookup = jnp.concatenate([init_means * inverse, -0.5 * inverse], axis=1)
    offsets = jnp.log(init_mass) - 0.5 * jnp.sum(
        jnp.log(init_vars) + init_means * init_means * inverse, axis=1
    )
    start_moment = jnp.concatenate(
        [
            init_mass[:, None] * init_means,
            init_mass[:, None] * (init_vars + init_means * init_means),
        ],
        axis=1,
    )
    return (lookup, offsets, start_moment)


def point_weights(assign_row, plan_row):
    step_size = 1.0 / plan_row.astype(jnp.float32)
    retain = 1.0 - step_size
    inclusive = jnp.flip(jnp.cumprod(jnp.flip(retain)))
    later_keep = jnp.concatenate([inclusive[1:], jnp.ones((1,), jnp.float32)])
    onehot = (
        assign_row[:, None] == jnp.arange(plan_row.shape[0], dtype=jnp.int32)[None, :]
    ).astype(jnp.float32)
    counts = jnp.sum(onehot, axis=0)
    batch_weight = step_size * later_keep / counts
    return (jnp.sum(onehot * batch_weight[None, :], axis=1), inclusive[0])


def maximize(mass_stat, moment_stat):
    half_width = moment_stat.shape[1] // 2
    centers = moment_stat[:, :half_width] / mass_stat[:, None]
    spreads = moment_stat[:, half_width:] / mass_stat[:, None] - centers * centers + VAR_PRIOR
    return (jnp.log(mass_stat), centers, spreads)


def join_partial(first_part, second_part):
    joined_peak = jnp.maximum(first_part[0], second_part[0])
    joined_total = first_part[1] * jnp.exp(first_part[0] - joined_peak) + second_part[1] * jnp.exp(
        second_part[0] - joined_peak
    )
    return (joined_peak, joined_total)


def compose_affine(first_part, second_part):
    return (
        first_part[0] * second_part[0],
        second_part[0] * first_part[1] + second_part[1],
        second_part[0] * first_part[2] + second_part[2],
    )


def multiply_pair(first_part, second_part):
    return first_part * second_part


def local(points, assign, plan, init_mass, init_means, init_vars):
    lookup, offsets, start_moment = prepare(init_mass, init_means, init_vars)
    features = jnp.concatenate([points, points * points], axis=1)
    logits = (
        lax.dot_general(
            features,
            lookup,
            (((1,), (1,)), ((), ())),
            precision=best_precision,
            preferred_element_type=jnp.float32,
        )
        + offsets[None, :]
    )
    local_peak = jnp.max(logits, axis=1)
    exponent = jnp.exp(logits - local_peak[:, None])
    local_total = jnp.sum(exponent, axis=1)
    row_peak, row_total = merged((local_peak, local_total), "comp", join_partial)
    responsibility = exponent * (jnp.exp(local_peak - row_peak) / row_total)[:, None]
    weight_row, decay_all = point_weights(assign[0], plan[0])
    weighted = responsibility * weight_row[:, None]
    mass_term = jnp.sum(weighted, axis=0)
    moment_term = lax.dot_general(
        weighted,
        features,
        (((0,), (0,)), ((), ())),
        precision=best_precision,
        preferred_element_type=jnp.float32,
    )
    unit_scalar = jnp.ones((), jnp.float32)
    before, prior_mass, prior_moment = carried_in(
        (decay_all, mass_term, moment_term),
        SEQ,
        compose_affine,
        (unit_scalar, jnp.zeros_like(mass_term), jnp.zeros_like(moment_term)),
    )
    entry_mass = before * init_mass + prior_mass
    entry_moment = before * start_moment + prior_moment
    mass_stat = decay_all * entry_mass + mass_term
    moment_stat = decay_all * entry_moment + moment_term
    logmass, centers, spreads = maximize(mass_stat, moment_stat)
    after = carried_in_2(decay_all, SEQ, multiply_pair, unit_scalar)
    total_mass, total_moment = together(
        (after * mass_term, after * moment_term), (("seq_0", "seq_1"), "seq_2")
    )
    whole_decay = before * decay_all * after
    final_logmass, final_means, final_vars = maximize(
        whole_decay * init_mass + total_mass, whole_decay * start_moment + total_moment
    )
    return (
        logmass[None],
        centers[None],
        spreads[None],
        final_logmass[None],
        final_means[None],
        final_vars[None],
    )


def solution(mesh):
    split = Mesh(
        mesh.devices.reshape(8, 4, 2, mesh.shape["comp"]), ("seq_0", "seq_1", "seq_2", "comp")
    )
    return jax.shard_map(
        local,
        mesh=split,
        in_specs=(
            P(SEQ, None),
            P(SEQ, None),
            P(SEQ, None),
            P("comp"),
            P("comp", None),
            P("comp", None),
        ),
        out_specs=(
            P(SEQ, "comp"),
            P(SEQ, "comp", None),
            P(SEQ, "comp", None),
            P(SEQ, "comp"),
            P(SEQ, "comp", None),
            P(SEQ, "comp", None),
        ),
        check_vma=False,
    )
```

profile of v0, /device:TPU:1, one launch (start us, length us, event | category | flops | bytes accessed | tf_op | source)
XLA Modules:
  0.0 231.2 jit_solution(16486741577411086647)
XLA Ops:
  7.2 1.2 add_multiply_fusion
  8.4 0.7 multiply_subtract_fusion
  9.1 2.6 %mul.456 = f32[2048,256]{1,0:T(8,128)S(1)} multiply(f32[2048,256]{1,0:T(8,128)} %param.6, f32[2048,256]{1,0:T(8,128)} %param.6) | non-fusion elementwise | flops 524288 | bytes 6291456 | tf_op jit(solution)/shard_map/mul | solution.py:195
  11.7 0.2 copy-done
  11.9 3.9 %fusion.55 = (f32[2048]{0:T(1024)S(1)}, f32[2048,256]{0,1:T(8,128)S(1)}) fusion(f32[256]{0:T(256)S(1)} %multiply_subtract_fusion, f32[256,256]{1,0:T(8,128)S(1)} %get-tuple-element.27, f32[256,256]{1,0:T(8,128)S(1)} %get-tuple-element.24, f32[2048,256]{1,0:T(8,128)S(1)} %mul.456, f32[2048,256]{1,0:T(8,128)S(1)} %copy-done), kind=kOutput, calls=%fused_computation.133 | convolution fusion | flops 3223451648 | bytes 6824960 | tf_op jit(solution)/shard_map/dot_general | solution.py:197
  15.9 1.3 copy-done.1
  17.2 0.3 fusion.3
  17.6 0.6 broadcast_in_dim.75
  18.2 4.8 %all-to-all-start = ((f32[4,2,2048]{2,1,0:T(2,128)}), f32[4,2,2048]{2,1,0:T(2,128)S(1)}, u32[]{:S(2)}, u32[]{:S(2)}) async-start(f32[4,2,2048]{2,1,0:T(2,128)} %broadcast_in_dim.75), calls=%async_computation | async-start | bytes 131072 | tf_op jit(solution)/shard_map/all_to_all | solution.py:16
  23.0 0.1 convert_reduce_fusion
  23.3 0.2 reduce-window.4
  23.8 3.8 %all-to-all-done = f32[4,2,2048]{2,1,0:T(2,128)S(1)} async-done(((f32[4,2,2048]{2,1,0:T(2,128)}), f32[4,2,2048]{2,1,0:T(2,128)S(1)}, u32[]{:S(2)}, u32[]{:S(2)}) %all-to-all-start) | async-done | bytes 65568 | tf_op jit(solution)/shard_map/all_to_all | solution.py:16
  27.9 7.0 %fusion = f32[256,512]{1,0:T(8,128)} fusion(f32[2048,256]{1,0:T(8,128)} %copy-done.3, f32[2048,256]{1,0:T(8,128)S(1)} %copy-done, f32[2048,256]{0,1:T(8,128)} %copy-done.1, f32[2048]{0:T(1024)S(1)} %select_reduce_fusion, f32[2048]{0:T(1024)S(1)} %exponential_divide_fusion, f32[2048]{0:T(1024)S(1)} %get-tuple-element.50), kind=kOutput, calls=%fused_computation.1 | convolution fusion | flops 3223846912 | bytes 6840320 | tf_op jit(solution)/shard_map/dot_general | solution.py:214
  34.9 0.6 slice.238
  35.5 0.6 dynamic-slice
  36.1 1.3 bitcast_dynamic-update-slice_fusion
  37.4 4.9 %all-reduce = f32[2]{0:T(128)S(1)} all-reduce(f32[2]{0:T(128)S(1)} %bitcast_dynamic-update-slice_fusion), channel_id=2, replica_groups=mesh['seq_0'=8,'seq_1'=4,'seq_2'=2,'comp'=4] {'seq_2'}, use_global_device_ids=true, to_apply=%add | all-reduce | flops 2 | bytes 16
  42.3 0.6 fusion.54
  43.6 9.1 %all-gather.14.cloned.1.call-done = f32[512,512]{1,0:T(8,128)} async-done(((f32[256,512]{1,0:T(8,128)}), f32[512,512]{1,0:T(8,128)}) %all-gather.14.cloned.1.call-update) | async-done | bytes 1048592 | tf_op jit(solution)/shard_map/all_gather | solution.py:60
  52.7 2.7 %fusion.15 = f32[1,256,512]{2,1,0:T(8,128)} fusion(f32[512,512]{1,0:T(8,128)} %all-gather.14.cloned.1.call-done, f32[]{:T(128)} %bitcast.6, f32[]{:T(128)S(6)} %mul.455), kind=kLoop, calls=%fused_computation.32 | loop fusion | flops 393216 | bytes 1572872 | tf_op jit(solution)/shard_map/add | solution.py:185
  56.8 0.6 dynamic-slice.1
  57.4 0.8 dynamic-update-slice.1
  58.2 8.2 %all-reduce.1 = f32[4]{0:T(128)S(1)} all-reduce(f32[4]{0:T(128)S(1)} %dynamic-update-slice.1), channel_id=1, replica_groups=mesh['seq_0'=8,'seq_1'=4,'seq_2'=2,'comp'=4] {'seq_1'}, use_global_device_ids=true, to_apply=%add.1 | all-reduce | flops 4 | bytes 32
  66.3 0.7 fusion.53
  67.7 21.7 %all-gather.10.cloned.1.call-done = f32[4,256,512]{2,1,0:T(8,128)} async-done(((f32[1,256,512]{2,1,0:T(8,128)}), f32[4,256,512]{2,1,0:T(8,128)}) %all-gather.10.cloned.1.call-update) | async-done | bytes 2097168 | tf_op jit(solution)/shard_map/all_gather | solution.py:60
  89.3 4.6 %slice_add_fusion.8 = f32[1,256,512]{2,1,0:T(8,128)} fusion(f32[4,256,512]{2,1,0:T(8,128)} %all-gather.10.cloned.1.call-done, f32[]{:T(128)} %bitcast.11, f32[]{:T(128)} %bitcast.12, f32[]{:T(128)S(6)} %mul.453, f32[]{:T(128)} %bitcast.10), kind=kLoop, calls=%fused_computation.27 | loop fusion | flops 917504 | bytes 2621456 | tf_op jit(solution)/shard_map/add | solution.py:185
  93.9 1.3 broadcast_in_dim.83
  95.2 9.6 %all-to-all-start.1 = ((f32[64,1,1]{2,1,0:T(1,128)}), f32[64,1,1]{2,1,0:T(1,128)S(1)}, u32[]{:S(2)}, u32[]{:S(2)}) async-start(f32[64,1,1]{2,1,0:T(1,128)} %broadcast_in_dim.83), calls=%async_computation.1 | async-start | bytes 65536 | tf_op jit(solution)/shard_map/all_to_all | solution.py:16
  106.1 0.6 dynamic-slice.2
  107.9 0.7 dynamic-update-slice.2
  108.6 15.7 %all-reduce.2 = f32[8]{0:T(128)S(1)} all-reduce(f32[8]{0:T(128)S(1)} %dynamic-update-slice.2), channel_id=1, replica_groups=mesh['seq_0'=8,'seq_1'=4,'seq_2'=2,'comp'=4] {'seq_0'}, use_global_device_ids=true, to_apply=%add.2 | all-reduce | flops 8 | bytes 64
  125.6 0.6 reduce.1
  126.2 0.1 slice.299
  126.3 0.1 slice.297
  126.7 0.1 slice.302
  127.5 0.6 fusion.51
  129.4 0.1 copy.25
  129.6 0.5 fusion.4
  130.2 0.6 reshape_reshape.6
  130.8 6.3 %all_to_all.39 = f32[2,32,2052]{2,1,0:T(8,128)S(1)} all-to-all(f32[2,32,2052]{2,1,0:T(8,128)S(1)} %copy.20), channel_id=1, replica_groups=mesh['seq_0'=8,'seq_1'=4,'seq_2'=2,'comp'=4] {'seq_2'}, dimensions={0} | all-to-all | bytes 1050624 | tf_op jit(solution)/shard_map/all_to_all | solution.py:92
  137.2 0.9 all_to_all.29
  138.0 7.3 %all-to-all-start.3 = ((f32[32,1,2052]{2,1,0:T(1,128)}), f32[32,1,2052]{2,1,0:T(1,128)S(1)}, u32[]{:S(2)}, u32[]{:S(2)}) async-start(f32[32,1,2052]{2,1,0:T(1,128)} %all_to_all.29), calls=%async_computation.3 | async-start | bytes 557056 | tf_op jit(solution)/shard_map/all_to_all | solution.py:99
  145.4 0.7 fusion.52
  153.3 2.1 all-gather.3
  155.4 0.6 broadcast_select_fusion
  156.0 8.0 %all-gather.4 = f32[4,1,256]{2,1,0:T(1,128)S(1)} all-gather(f32[1,1,256]{2,1,0:T(1,128)S(1)} %get-tuple-element.31), channel_id=1, replica_groups=mesh['seq_0'=8,'seq_1'=4,'seq_2'=2,'comp'=4] {'seq_1'}, dimensions={0}, use_global_device_ids=true | all-gather | bytes 5120 | tf_op jit(solution)/shard_map/all_gather | solution.py:60
  164.0 0.2 reduce_sum.72
  164.2 0.8 broadcast_in_dim.85
  165.0 7.1 %all-to-all-start.4 = ((f32[32,1,2052]{2,1,0:T(1,128)}), f32[32,1,2052]{2,1,0:T(1,128)S(1)}, u32[]{:S(2)}, u32[]{:S(2)}) async-start(f32[32,1,2052]{2,1,0:T(1,128)} %broadcast_in_dim.85), calls=%async_computation.4 | async-start | bytes 557056 | tf_op jit(solution)/shard_map/all_to_all | solution.py:16
  172.1 1.9 multiply_add_fusion.2
  174.0 13.4 %all-gather.5 = f32[8,1,256]{2,1,0:T(1,128)S(1)} all-gather(f32[1,1,256]{2,1,0:T(1,128)S(1)} %bitcast.188), channel_id=1, replica_groups=mesh['seq_0'=8,'seq_1'=4,'seq_2'=2,'comp'=4] {'seq_0'}, dimensions={0}, use_global_device_ids=true | all-gather | bytes 9216 | tf_op jit(solution)/shard_map/all_gather | solution.py:60
  187.3 4.5 %broadcast_multiply_fusion.2 = (f32[1,256]{1,0:T(1,128)S(1)}, f32[1,256]{1,0:T(1,128)S(1)}, f32[1,256]{1,0:T(1,128)S(1)}) fusion(f32[]{:T(128)} %bitcast.22, f32[8,1,256]{2,1,0:T(1,128)S(1)} %all-gather.5, f32[]{:T(128)} %bitcast.21, f32[]{:T(128)} %bitcast.19, f32[]{:T(128)} %bitcast.20, f32[]{:T(128)S(6)} %mul.448, f32[]{:T(128)} %bitcast.16, ...), kind=kLoop, calls=%fused_computation.118 | loop fusion | flops 3584 | bytes 10272 | tf_op jit(solution)/shard_map/mul | solution.py:184
  191.9 2.6 %broadcast_select_fusion.3 = f32[1,256]{1,0:T(1,128)S(1)} fusion(pred[]{:T(512)S(6)} %gt.49, f32[1,256]{1,0:T(1,128)S(1)} %get-tuple-element.11, pred[]{:T(512)S(6)} %gt.50, f32[1,256]{1,0:T(1,128)S(1)} %get-tuple-element.12, pred[]{:T(512)S(6)} %gt.55, pred[]{:T(512)S(6)} %gt.54, pred[]{:T(512)S(6)} %gt.53, pred[]{:T(512)S(6)} %gt.52, pred[]{:T(512)S(6)} %gt.51, ...), kind=kLoop, calls=%fused_computation.76 | loop fusion | flops 4096 | bytes 8219 | tf_op jit(solution)/shard_map/jit(_where)/select_n | solution.py:65
  194.5 9.4 %all_to_all.40 = f32[2,32,2052]{2,1,0:T(8,128)S(1)} all-to-all(f32[2,32,2052]{2,1,0:T(8,128)S(1)} %broadcast_in_dim.87), channel_id=1, replica_groups=mesh['seq_0'=8,'seq_1'=4,'seq_2'=2,'comp'=4] {'seq_2'}, dimensions={0} | all-to-all | bytes 1050624 | tf_op jit(solution)/shard_map/all_to_all | solution.py:16
  204.0 0.4 copy.21
  204.4 0.5 reshape_reshape.7
  204.9 0.8 copy-done.6
  205.8 0.8 slice.374
  206.6 2.1 reshape.149
  208.7 1.9 fusion.45
  210.6 1.1 multiply_add_fusion
  211.7 0.9 fusion.22
  212.6 11.2 %fusion.14 = f32[256,512]{1,0:T(8,128)S(1)} fusion(f32[256,512]{1,0:T(8,128)S(1)} %copy-done.5, f32[8,256,512]{2,1,0:T(8,128)} %all-gather.12.cloned.1.call-done, f32[512,512]{1,0:T(8,128)} %all-gather.14.cloned.1.call-done, f32[4,256,512]{2,1,0:T(8,128)S(1)} %copy-done.4, f32[256,256]{1,0:T(8,128)S(1)} %get-tuple-element.23, ...), kind=kLoop, calls=%fused_computation.19 | loop fusion | flops 6291456 | bytes 8912982 | tf_op jit(solution)/shard_map/add | solution.py:231
  223.8 0.9 fusion.25
  (77 shorter events, 2.0 us)
Async XLA Ops:
  9.1 2.9 %copy-start = (f32[2048,256]{1,0:T(8,128)S(1)}, f32[2048,256]{1,0:T(8,128)}, u32[]{:S(2)}) copy-start(f32[2048,256]{1,0:T(8,128)} %param.6) | copy-start | bytes 6291460
  11.7 4.1 %copy-start.3 = (f32[2048,256]{1,0:T(8,128)}, f32[2048,256]{1,0:T(8,128)S(1)}, u32[]{:S(2)}) copy-start(f32[2048,256]{1,0:T(8,128)S(1)} %mul.456) | copy-start | bytes 6291460
  15.9 1.4 copy-start.1
  15.9 7.2 %copy-start.7 = (s32[1,2048]{1,0:T(1,128)S(1)}, s32[1,2048]{1,0:T(1,128)}, u32[]{:S(2)}) copy-start(s32[1,2048]{1,0:T(1,128)} %param.7) | copy-start | bytes 24580
  15.9 7.3 %copy-start.9 = (s32[1,4]{1,0:T(1,128)S(1)}, s32[1,4]{1,0:T(1,128)}, u32[]{:S(2)}) copy-start(s32[1,4]{1,0:T(1,128)} %param.8) | copy-start | bytes 52
  18.2 9.3 %all-to-all-start = ((f32[4,2,2048]{2,1,0:T(2,128)}), f32[4,2,2048]{2,1,0:T(2,128)S(1)}, u32[]{:S(2)}, u32[]{:S(2)}) async-start(f32[4,2,2048]{2,1,0:T(2,128)} %broadcast_in_dim.75), calls=%async_computation | async-start | bytes 131072 | tf_op jit(solution)/shard_map/all_to_all | solution.py:16
  23.0 29.6 %all-gather.14.cloned.1.call-start = ((), (), s32[]{:S(2)}) async-start(), calls=%async_computation.8 | async-start | bytes 1572864 | tf_op jit(solution)/shard_map/all_gather | solution.py:60
  27.8 7.7 %copy-start.12 = (u32[256]{0:T(256)S(1)}, u32[256]{0:T(256)}, u32[]{:S(2)}) copy-start(u32[256]{0:T(256)} %constant.60) | copy-start | bytes 3076
  34.9 22.0 %copy-start.11 = (u32[256]{0:T(256)S(1)}, u32[256]{0:T(256)}, u32[]{:S(2)}) copy-start(u32[256]{0:T(256)} %constant.65) | copy-start | bytes 3076
  34.9 54.5 %all-gather.10.cloned.1.call-start = ((), (), s32[]{:S(2)}) async-start(), calls=%async_computation.6 | async-start | bytes 2621440 | tf_op jit(solution)/shard_map/all_gather | solution.py:60
  55.4 50.6 %copy-start.10 = (u32[256]{0:T(256)S(1)}, u32[256]{0:T(256)}, u32[]{:S(2)}) copy-start(u32[256]{0:T(256)} %constant.70) | copy-start | bytes 3076
  55.4 74.0 %copy-start.5 = (f32[256,512]{1,0:T(8,128)S(1)}, f32[256,512]{1,0:T(8,128)}, u32[]{:S(2)}) copy-start(f32[256,512]{1,0:T(8,128)} %fusion) | copy-start | bytes 1572868
  55.4 157.2 %all-gather.12.cloned.1.call-start = ((), (), s32[]{:S(2)}) async-start(), calls=%async_computation.7 | async-start | bytes 4718592 | tf_op jit(solution)/shard_map/all_gather | solution.py:60
  89.3 40.2 %copy-start.2 = (f32[2048,256]{0,1:T(8,128)S(1)}, f32[2048,256]{0,1:T(8,128)}, u32[]{:S(2)}) copy-start(f32[2048,256]{0,1:T(8,128)} %copy-done.1) | copy-start | bytes 6291460
  95.2 30.4 %all-to-all-start.1 = ((f32[64,1,1]{2,1,0:T(1,128)}), f32[64,1,1]{2,1,0:T(1,128)S(1)}, u32[]{:S(2)}, u32[]{:S(2)}) async-start(f32[64,1,1]{2,1,0:T(1,128)} %broadcast_in_dim.83), calls=%async_computation.1 | async-start | bytes 65536 | tf_op jit(solution)/shard_map/all_to_all | solution.py:16
  138.0 25.9 %all-to-all-start.3 = ((f32[32,1,2052]{2,1,0:T(1,128)}), f32[32,1,2052]{2,1,0:T(1,128)S(1)}, u32[]{:S(2)}, u32[]{:S(2)}) async-start(f32[32,1,2052]{2,1,0:T(1,128)} %all_to_all.29), calls=%async_computation.3 | async-start | bytes 557056 | tf_op jit(solution)/shard_map/all_to_all | solution.py:99
  165.0 29.4 %all-to-all-start.4 = ((f32[32,1,2052]{2,1,0:T(1,128)}), f32[32,1,2052]{2,1,0:T(1,128)S(1)}, u32[]{:S(2)}, u32[]{:S(2)}) async-start(f32[32,1,2052]{2,1,0:T(1,128)} %broadcast_in_dim.85), calls=%async_computation.4 | async-start | bytes 557056 | tf_op jit(solution)/shard_map/all_to_all | solution.py:16
  204.0 4.7 %copy-start.8 = (f32[256]{0:T(256)S(1)}, f32[256]{0:T(256)}, u32[]{:S(2)}) copy-start(f32[256]{0:T(256)} %param.9) | copy-start | bytes 3076
  204.9 0.8 copy-start.6
  206.6 6.0 %copy-start.4 = (f32[4,256,512]{2,1,0:T(8,128)S(1)}, f32[4,256,512]{2,1,0:T(8,128)}, u32[]{:S(2)}) copy-start(f32[4,256,512]{2,1,0:T(8,128)} %all-gather.10.cloned.1.call-done) | copy-start | bytes 6291460
Sparse Core Ops, SparseCore 0:
  35.0 17.6 all-gather.13
  55.5 33.7 all-gather.9
  94.0 55.7 all-gather.11
where the time goes:
time: 233 us; the launch traced here: 231 us
  blocking collectives  68 us (29%)
  other arithmetic  39.8 us (17%)
  waiting for transfers between devices  34.6 us (15%)
  between operations  29.1 us (12%)
  starting transfers between devices  28.9 us (12%)
  local copies, waits for them, and re-layouts  19.9 us (9%)
  matrix products  10.9 us (5%)
    all_gather x3, waiting for transfers between devices, carried_in(): pieces = jax.tree.map(lambda part: lax.all_gather(part, axis), so_far)  30.8 us
    unnamed x3, blocking collectives  28.8 us
    all_gather x3, blocking collectives, carried_in(): pieces = jax.tree.map(lambda part: lax.all_gather(part, axis), so_far)  23.4 us
    all_to_all x3, starting transfers between devices, copy_for_each(): lax.all_to_all(jnp.broadcast_to(x[None], (length, *x.shape)), axis, 0, 0,...  21.5 us
    add x1, other arithmetic, local(): moment_stat = decay_all * entry_moment + moment_term  11.2 us
    all_to_all x1, blocking collectives, copy_for_each(): lax.all_to_all(jnp.broadcast_to(x[None], (length, *x.shape)), axis, 0, 0,...  9.45 us
    all_to_all x1, starting transfers between devices, sum_by_axis(): return jnp.sum(lax.all_to_all(own, far, 0, 0, tiled=True), axis=0)  7.35 us
    add x2, other arithmetic, compose_affine(): second_part[0] * first_part[2] + second_part[2]  7.28 us
  transfers between devices with their start and end apart: 7, of which 3 were waited for; matrix products, arithmetic and copies ran while one was open for 14% of the time, Pallas kernels for 0%

commit v1 on v0

v1 whole, which is shorter than its diff:
```python
import functools

import jax
import jax.numpy as jnp
from jax import lax
from jax.experimental import pallas as pl
from jax.experimental.pallas import tpu as pltpu
from jax.sharding import Mesh
from jax.sharding import PartitionSpec as P

SEQ = ("seq_0", "seq_1", "seq_2")
MESH = pl.DeviceIdType.MESH
VAR_PRIOR = 0.01
BLOCK = 512


def split3(a):
    hi = a.astype(jnp.bfloat16)
    rest = a - hi.astype(jnp.float32)
    mid = rest.astype(jnp.bfloat16)
    low = (rest - mid.astype(jnp.float32)).astype(jnp.bfloat16)
    return hi, mid, low


def dot_nt(a, b):
    return lax.dot_general(a, b, (((1,), (1,)), ((), ())), preferred_element_type=jnp.float32)


def dot_nn(a, b):
    return lax.dot_general(a, b, (((1,), (0,)), ((), ())), preferred_element_type=jnp.float32)


def drain(ref, sem):
    pltpu.make_async_copy(ref, ref, sem).wait()


def kernel(
    nz, ny, nx,
    pts, asg, plan, mass_in, means, varis,
    dlog, dmean, dvar, flog, fmean, fvar,
    look, feat1, feat2, expo, wsplit, wrow, mcol,
    stat, statin, mine, other, partner, pair_small, small, smallbuf,
    term, inbuf, outbuf, carrybuf, total, state, stateout,
    x_send, x_recv, pair_send, pair_recv, in_send, in_recv, sm_send, sm_recv,
    carry_send, carry_recv, t1_send, t1_recv, t2_send, t2_recv,
):
    z, y, c, x = (lax.axis_index(n) for n in (*SEQ, "comp"))
    nc = nz * ny
    kl, width = means.shape
    share = kl // nc
    blocks = pts.shape[0] // BLOCK
    here = z * ny + y
    own = y * nz + z

    def owned(q):
        return lax.rem(q, ny) * nz + q // ny

    def chip(q):
        return {"seq_0": q // ny, "seq_1": lax.rem(q, ny)}

    def rows(o):
        return pl.ds(pl.multiple_of(o * share, share), share)

    mate = {"seq_2": 1 - c}

    barrier = pltpu.get_barrier_semaphore()

    @pl.loop(1, nc)
    def _(k):
        pl.semaphore_signal(barrier, inc=1, device_id=chip(lax.rem(here + k, nc)), device_id_type=MESH)

    pl.semaphore_signal(barrier, inc=1, device_id=mate, device_id_type=MESH)
    for k in range(1, nx):
        pl.semaphore_signal(barrier, inc=1, device_id={"comp": lax.rem(x + k, nx)}, device_id_type=MESH)

    mu, var = means[...], varis[...]
    inverse = 1.0 / var
    for h, table in enumerate((mu * inverse, -0.5 * inverse)):
        for part, piece in enumerate(split3(table)):
            look[part, :, h * width : (h + 1) * width] = piece
    diagonal = lax.broadcasted_iota(jnp.int32, (kl, kl), 0) == lax.broadcasted_iota(jnp.int32, (kl, kl), 1)

    def column(row):
        return jnp.sum(jnp.where(diagonal, row, 0.0), axis=1, keepdims=True)

    def row_of(col):
        return jnp.sum(jnp.where(diagonal, col, 0.0), axis=0, keepdims=True)

    start_col = column(mass_in[...])
    mcol[...] = jnp.broadcast_to(start_col, mcol.shape)
    offset = jnp.log(start_col) - 0.5 * jnp.sum(jnp.log(var) + mu * mu * inverse, axis=1, keepdims=True)

    steps = 1.0 / plan[...].astype(jnp.float32)
    keep = jnp.ones((1, 1), jnp.float32)
    weight = jnp.zeros(asg.shape, jnp.float32)
    for m in range(plan.shape[1] - 1, -1, -1):
        step = steps[:, m : m + 1]
        chosen = asg[...] == m
        count = jnp.sum(jnp.where(chosen, 1.0, 0.0), axis=1, keepdims=True)
        weight = jnp.where(chosen, step * keep / count, weight)
        keep = keep * (1.0 - step)
    decay_row = jnp.broadcast_to(keep, (1, kl))
    for b in range(blocks):
        wrow[b] = weight[:, b * BLOCK : (b + 1) * BLOCK]

    for b in range(blocks):
        p = pts[b * BLOCK : (b + 1) * BLOCK, :]
        logits = None
        thirds = []
        for h, f in enumerate((p, p * p)):
            hi, mid, low = split3(f)
            feat1[h, b] = hi
            feat2[h, b] = mid
            thirds.append((hi, mid, low))
        hi, mid, low = (jnp.concatenate([thirds[0][i], thirds[1][i]], axis=1) for i in range(3))
        logits = dot_nt(hi, look[2]) + dot_nt(low, look[0]) + dot_nt(mid, look[1])
        logits = logits + dot_nt(hi, look[1]) + dot_nt(mid, look[0]) + dot_nt(hi, look[0])
        logits = logits.T + offset
        peak = jnp.max(logits, axis=0, keepdims=True)
        e = jnp.exp(logits - peak)
        expo[b] = e
        stat[b, 0:1, :] = peak
        stat[b, 1:2, :] = jnp.sum(e, axis=0, keepdims=True)
        if b == 0:
            pl.semaphore_wait(barrier, nc - 1 + 1 + nx - 1)
        for k in range(1, nx):
            pltpu.make_async_remote_copy(
                stat.at[b], statin.at[k - 1, b], x_send.at[k - 1, b], x_recv.at[k - 1, b],
                device_id={"comp": lax.rem(x + k, nx)}, device_id_type=MESH,
            ).start()

    mass = jnp.zeros((kl, 1), jnp.float32)
    acc = jnp.zeros((kl, width), jnp.float32)
    for b in range(blocks):
        for k in range(1, nx):
            pltpu.make_async_remote_copy(
                stat.at[b], statin.at[k - 1, b], x_send.at[k - 1, b], x_recv.at[k - 1, b],
                device_id={"comp": lax.rem(x + k, nx)}, device_id_type=MESH,
            ).wait()
        near = stat[b, 0:1, :]
        peaks = [near] + [statin[k, b, 0:1, :] for k in range(nx - 1)]
        sums = [stat[b, 1:2, :]] + [statin[k, b, 1:2, :] for k in range(nx - 1)]
        peak = functools.reduce(jnp.maximum, peaks)
        whole = sum(s * jnp.exp(q - peak) for q, s in zip(peaks, sums))
        scale = jnp.exp(near - peak) / whole * wrow[b]
        w = expo[b] * scale
        mass = mass + jnp.sum(w, axis=1, keepdims=True)
        w1 = w.astype(jnp.bfloat16)
        w2 = (w - w1.astype(jnp.float32)).astype(jnp.bfloat16)
        wsplit[0, b] = w1
        wsplit[1, b] = w2
        f1, f2 = feat1[1 - c, b], feat2[1 - c, b]
        acc = acc + dot_nn(w2, f1) + dot_nn(w1, f2) + dot_nn(w1, f1)
    other[...] = acc
    to_mate = pltpu.make_async_remote_copy(
        other, partner, pair_send.at[0], pair_recv.at[0], device_id=mate, device_id_type=MESH
    )
    to_mate.start()
    pair_small[c, 0:1, :] = row_of(mass)
    pair_small[c, 1:2, :] = decay_row
    small_mate = pltpu.make_async_remote_copy(
        pair_small.at[c], pair_small.at[c], pair_send.at[1], pair_recv.at[1], device_id=mate, device_id_type=MESH
    )
    small_mate.start()
    acc = jnp.zeros((kl, width), jnp.float32)
    for b in range(blocks):
        w1, w2 = wsplit[0, b], wsplit[1, b]
        f1, f2 = feat1[c, b], feat2[c, b]
        acc = acc + dot_nn(w2, f1) + dot_nn(w1, f2) + dot_nn(w1, f1)
    mine[...] = acc
    small_mate.wait()
    to_mate.wait()

    first_core = c == 0
    decay0, decay1 = pair_small[0, 1:2, :], pair_small[1, 1:2, :]
    one = jnp.ones_like(decay0)
    term[...] = jnp.where(first_core, decay1, one) * acc + jnp.where(first_core, one, decay1) * partner[...]
    small[0:1, :] = decay1 * pair_small[0, 0:1, :] + pair_small[1, 0:1, :]
    small[1:2, :] = decay0 * decay1

    @pl.loop(1, nc)
    def _(k):
        q = lax.rem(here + k, nc)
        pltpu.make_async_remote_copy(
            small, smallbuf.at[here], sm_send, sm_recv, device_id=chip(q), device_id_type=MESH
        ).start()
        pltpu.make_async_remote_copy(
            term.at[rows(owned(q))], inbuf.at[here], in_send, in_recv, device_id=chip(q), device_id_type=MESH
        ).start()

    inbuf[here] = term[rows(own), :]
    smallbuf[here] = small[...]
    mu_own, var_own = means[rows(own), :], varis[rows(own), :]
    s = mcol[rows(own), 0:1] * jnp.where(first_core, mu_own, var_own + mu_own * mu_own)
    ms = mass_in[...]
    drain(smallbuf.at[pl.ds(0, nc - 1)], sm_recv)
    drain(inbuf.at[pl.ds(0, nc - 1)], in_recv)

    def advance(q, held):
        s, ms, entry = held
        entry = jnp.where(q == here, ms, entry)
        outbuf[q] = s
        decay = smallbuf[q, 1:2, :]
        return decay * s + inbuf[q], decay * ms + smallbuf[q, 0:1, :], entry

    s, ms, entry_mass = lax.fori_loop(0, nc, advance, (s, ms, ms), unroll=4)
    total[c, rows(own), :] = s

    for k in range(1, nz):
        pltpu.make_async_remote_copy(
            total.at[c, rows(own)], total.at[c, rows(own)], t1_send, t1_recv,
            device_id={"seq_0": lax.rem(z + k, nz)}, device_id_type=MESH,
        ).start()

    @pl.loop(1, nc)
    def _(k):
        q = lax.rem(here + k, nc)
        pltpu.make_async_remote_copy(
            outbuf.at[q], carrybuf.at[rows(own)], carry_send, carry_recv, device_id=chip(q), device_id_type=MESH
        ).start()

    carrybuf[rows(own), :] = outbuf[here]
    drain(total.at[0, pl.ds(0, (nz - 1) * share)], t1_recv)
    line = pl.ds(pl.multiple_of(y * nz * share, nz * share), nz * share)
    for k in range(1, ny):
        pltpu.make_async_remote_copy(
            total.at[c, line], total.at[c, line], t2_send, t2_recv,
            device_id={"seq_1": lax.rem(y + k, ny)}, device_id_type=MESH,
        ).start()
    drain(total.at[0, pl.ds(0, (ny - 1) * nz * share)], t2_recv)
    total_mate = pltpu.make_async_remote_copy(
        total.at[c], total.at[c], pair_send.at[2], pair_recv.at[2], device_id=mate, device_id_type=MESH
    )
    total_mate.start()

    drain(carrybuf.at[pl.ds(0, (nc - 1) * share)], carry_recv)
    from_own, from_mate = mine[...], partner[...]
    state0 = decay0 * carrybuf[...] + jnp.where(first_core, from_own, from_mate)
    state1 = decay1 * state0 + jnp.where(first_core, from_mate, from_own)
    stateout[...] = jnp.where(first_core, state1, state0)
    state_mate = pltpu.make_async_remote_copy(
        stateout, state.at[c], pair_send.at[3], pair_recv.at[3], device_id=mate, device_id_type=MESH
    )
    state_mate.start()
    state[c] = jnp.where(first_core, state0, state1)
    mass0 = decay0 * entry_mass + pair_small[0, 0:1, :]
    mass1 = decay1 * mass0 + pair_small[1, 0:1, :]
    mass_row = jnp.where(first_core, mass0, mass1)
    dlog[...] = jnp.log(mass_row)
    flog[...] = jnp.log(ms)
    inv_dev, inv_final = 1.0 / column(mass_row), 1.0 / column(ms)

    total_mate.wait()
    centers = total[0] * inv_final
    fmean[...] = centers
    fvar[...] = total[1] * inv_final - centers * centers + VAR_PRIOR
    state_mate.wait()
    centers = state[0] * inv_dev
    dmean[...] = centers
    dvar[...] = state[1] * inv_dev - centers * centers + VAR_PRIOR

    drain(smallbuf.at[pl.ds(0, nc - 1)], sm_send)
    drain(inbuf.at[pl.ds(0, nc - 1)], in_send)
    drain(carrybuf.at[pl.ds(0, (nc - 1) * share)], carry_send)
    drain(total.at[0, pl.ds(0, (nz - 1) * share)], t1_send)
    drain(total.at[0, pl.ds(0, (ny - 1) * nz * share)], t2_send)


def local(nz, ny, nx, points, assign, plan, init_mass, init_means, init_vars):
    kl, width = init_means.shape
    count = points.shape[0]
    nc, blocks = nz * ny, count // BLOCK
    share = kl // nc
    f32, bf16 = jnp.float32, jnp.bfloat16
    vmem, dma = pltpu.VMEM, pltpu.SemaphoreType.DMA
    row, table = jax.ShapeDtypeStruct((1, kl), f32), jax.ShapeDtypeStruct((kl, width), f32)
    outs = pl.pallas_call(
        functools.partial(kernel, nz, ny, nx),
        out_shape=(row, table, table, row, table, table),
        in_specs=[pl.BlockSpec(memory_space=vmem)] * 6,
        out_specs=[pl.BlockSpec(memory_space=vmem)] * 6,
        scratch_shapes=[
            vmem((3, kl, 2 * width), bf16),
            vmem((2, blocks, BLOCK, width), bf16),
            vmem((2, blocks, BLOCK, width), bf16),
            vmem((blocks, kl, BLOCK), f32),
            vmem((2, blocks, kl, BLOCK), bf16),
            vmem((blocks, 1, BLOCK), f32),
            vmem((kl, 128), f32),
            vmem((blocks, 2, BLOCK), f32),
            vmem((nx - 1, blocks, 2, BLOCK), f32),
            vmem((kl, width), f32),
            vmem((kl, width), f32),
            vmem((kl, width), f32),
            vmem((2, 2, kl), f32),
            vmem((2, kl), f32),
            vmem((nc, 2, kl), f32),
            vmem((kl, width), f32),
            vmem((nc, share, width), f32),
            vmem((nc, share, width), f32),
            vmem((kl, width), f32),
            vmem((2, kl, width), f32),
            vmem((2, kl, width), f32),
            vmem((kl, width), f32),
            dma((nx - 1, blocks)), dma((nx - 1, blocks)),
            dma((4,)), dma((4,)),
            dma, dma, dma, dma, dma, dma, dma, dma, dma, dma,
        ],
        compiler_params=pltpu.CompilerParams(collective_id=0, has_side_effects=True, vmem_limit_bytes=60 * 2**20),
    )(points, assign, plan, init_mass.reshape(1, kl), init_means, init_vars)
    return tuple(o.reshape(1, kl) if o.shape[0] == 1 else o[None] for o in outs)


def solution(mesh):
    nz, ny, nx = 8, 4, mesh.shape["comp"]
    split = Mesh(mesh.devices.reshape(nz, ny, 2, nx), (*SEQ, "comp"))
    return jax.shard_map(
        functools.partial(local, nz, ny, nx),
        mesh=split,
        in_specs=(P(SEQ, None), P(SEQ, None), P(SEQ, None), P("comp"), P("comp", None), P("comp", None)),
        out_specs=(
            P(SEQ, "comp"), P(SEQ, "comp", None), P(SEQ, "comp", None),
            P(SEQ, "comp"), P(SEQ, "comp", None), P(SEQ, "comp", None),
        ),
        check_vma=False,
    )
```

time: 233 us -> 60.4 us (0.26)
  blocking collectives: 68 us -> 0 us
  Pallas kernels: 0 us -> 50.4 us
  other arithmetic: 39.8 us -> 0 us
  waiting for transfers between devices: 34.6 us -> 0 us
  starting transfers between devices: 28.9 us -> 0 us
  between operations: 29.1 us -> 0.64 us
  matrix products: 10.9 us -> 0 us
  local copies, waits for them, and re-layouts: 19.9 us -> 9.13 us
    pallas_call x0 -> x1, Pallas kernels: none -> 50.4 us  [local(): pl.pallas_call(functools.partial(kernel, nz, ny, nx), out_shape=(row, tab...]
    all_gather x3 -> x0, waiting for transfers between devices: 30.8 us -> none  [carried_in(): pieces = jax.tree.map(lambda part: lax.all_gather(part, axis), so_far)]
    all_to_all x4 -> x0, starting transfers between devices: 28.8 us -> none  [the longest x3 21.5 us: copy_for_each(): lax.all_to_all(jnp.broadcast_to(x[None], (length, *x.shape)), axis, 0, 0,...]
    unnamed x3 -> x0, blocking collectives: 28.8 us -> none
    all_gather x3 -> x0, blocking collectives: 23.4 us -> none  [carried_in(): pieces = jax.tree.map(lambda part: lax.all_gather(part, axis), so_far)]
    add x7 -> x0, other arithmetic: 21.5 us -> none  [the longest x1 11.2 us: local(): moment_stat = decay_all * entry_moment + moment_term]
    all_to_all x2 -> x0, blocking collectives: 15.8 us -> none  [the longest x1 9.45 us: copy_for_each(): lax.all_to_all(jnp.broadcast_to(x[None], (length, *x.shape)), axis, 0, 0,...]
    dot_general x2 -> x0, matrix products: 10.9 us -> none  [the longest x1 7 us: local(): lax.dot_general(weighted, features, (((0,), (0,)), ((), ())), precision=b...]
  transfers between devices with their start and end apart: 7 -> 0, of which waited for: 3 -> 0; matrix products, arithmetic and copies ran while one was open for 14% -> 0% of each run, Pallas kernels for 0% -> 0%
where the time goes in v1:
time: 60.4 us; the launch traced here: 60.1 us
  Pallas kernels  50.4 us (83%)
  local copies, waits for them, and re-layouts  9.13 us (15%)
  between operations  0.64 us (1%)
    pallas_call x1, Pallas kernels, local(): pl.pallas_call(functools.partial(kernel, nz, ny, nx), out_shape=(row, tab...  50.4 us
    unnamed x6, local copies, waits for them, and re-layouts  9.13 us

profile of v1, /device:TPU:1, one launch (start us, length us, event | category | flops | bytes accessed | tf_op | source)
XLA Modules:
  0.0 60.1 jit_solution(11994544828202687593)
XLA Ops:
  0.6 50.4 %shard_map.109 = (f32[1,256]{1,0:T(1,128)}, f32[256,256]{1,0:T(8,128)}, f32[256,256]{1,0:T(8,128)}, f32[1,256]{1,0:T(1,128)}, f32[256,256]{1,0:T(8,128)}, /*index=5*/f32[256,256]{1,0:T(8,128)}) custom-call(f32[2048,256]{1,0:T(8,128)} %pts.1, s32[1,2048]{1,0:T(1,128)} %asg.1, s32[1,4]{1,0:T(1,128)} %plan.1, f32[1,256]{1,0:T(1,128)} %bitcast.9, ...), custom_call_target="tpu_custom_call" | custom-call | tf_op jit(solution)/shard_map/pallas_call | solution.py:277
  51.0 1.2 %copy.18 = f32[1,256]{1,0:T(1,128)} copy(f32[1,256]{1,0:T(1,128)} %get-tuple-element.24) | data formatting | bytes 2048
  52.2 1.7 %copy.19 = f32[1,256,256]{2,1,0:T(8,128)} copy(f32[1,256,256]{2,1,0:T(8,128)} %bitcast.8) | data formatting | bytes 524288
  53.9 1.7 %copy.20 = f32[1,256,256]{2,1,0:T(8,128)} copy(f32[1,256,256]{2,1,0:T(8,128)} %bitcast.7) | data formatting | bytes 524288
  55.6 1.2 %copy.21 = f32[1,256]{1,0:T(1,128)} copy(f32[1,256]{1,0:T(1,128)} %get-tuple-element.27) | data formatting | bytes 2048
  56.8 1.7 %copy.22 = f32[1,256,256]{2,1,0:T(8,128)} copy(f32[1,256,256]{2,1,0:T(8,128)} %bitcast.6) | data formatting | bytes 524288
  58.5 1.7 %copy.23 = f32[1,256,256]{2,1,0:T(8,128)} copy(f32[1,256,256]{2,1,0:T(8,128)} %bitcast.5) | data formatting | bytes 524288

commit v2 on v1

v2 whole, which is shorter than its diff:
```python
import functools

import jax
import jax.numpy as jnp
from jax import lax
from jax.experimental import pallas as pl
from jax.experimental.pallas import tpu as pltpu
from jax.sharding import Mesh
from jax.sharding import PartitionSpec as P

SEQ = ("seq_0", "seq_1", "seq_2")
MESH = pl.DeviceIdType.MESH
VAR_PRIOR = 0.01
BLOCK = 512


def split3(a):
    hi = a.astype(jnp.bfloat16)
    rest = a - hi.astype(jnp.float32)
    mid = rest.astype(jnp.bfloat16)
    low = (rest - mid.astype(jnp.float32)).astype(jnp.bfloat16)
    return hi, mid, low


def dot_nt(a, b):
    return lax.dot_general(a, b, (((1,), (1,)), ((), ())), preferred_element_type=jnp.float32)


def dot_nn(a, b):
    return lax.dot_general(a, b, (((1,), (0,)), ((), ())), preferred_element_type=jnp.float32)


def drain(ref, sem):
    pltpu.make_async_copy(ref, ref, sem).wait()


def kernel(
    nz, ny, nx,
    pts_in, asg_in, plan_in, mass_from, means_in, varis_in,
    dlog, dmean, dvar, flog, fmean, fvar,
    pts, means, varis, asg, plan, mass_in, load,
    look, feat1, feat2, expo, wsplit, wrow, mcol,
    stat, statin, mine, other, partner, pair_decay, pair_mass, decay, decays, mass_out, masses,
    term, inbuf, outbuf, carrybuf, total, state, stateout,
    x_send, x_recv, pair_send, pair_recv, in_send, in_recv, mass_send, mass_recv, decay_send, decay_recv,
    carry_send, carry_recv, t1_send, t1_recv, t2_send, t2_recv,
):
    loads = [
        pltpu.make_async_copy(means_in, means, load.at[0]),
        pltpu.make_async_copy(varis_in, varis, load.at[1]),
        pltpu.make_async_copy(mass_from, mass_in, load.at[2]),
        pltpu.make_async_copy(asg_in, asg, load.at[3]),
        pltpu.make_async_copy(plan_in, plan, load.at[4]),
    ] + [
        pltpu.make_async_copy(pts_in.at[pl.ds(b * BLOCK, BLOCK)], pts.at[b], load.at[5 + b]) for b in range(pts.shape[0])
    ]
    for copy in loads:
        copy.start()
    z, y, c, x = (lax.axis_index(n) for n in (*SEQ, "comp"))
    nc = nz * ny
    kl, width = means.shape
    share = kl // nc
    blocks = pts.shape[0]
    here = z * ny + y
    own = y * nz + z

    def owned(q):
        return lax.rem(q, ny) * nz + q // ny

    def chip(q):
        return {"seq_0": q // ny, "seq_1": lax.rem(q, ny)}

    def rows(o):
        return pl.ds(pl.multiple_of(o * share, share), share)

    mate = {"seq_2": 1 - c}

    def away(offset, size):
        return min(offset, size - offset)

    offsets = [(dz, dy) for dz in range(nz) for dy in range(ny) if dz or dy]

    offsets.sort(key=lambda d: away(d[0], nz) + away(d[1], ny))
    others = [lax.rem(z + dz, nz) * ny + lax.rem(y + dy, ny) for dz, dy in offsets]

    barrier = pltpu.get_barrier_semaphore()

    @pl.loop(1, nc)
    def _(k):
        pl.semaphore_signal(barrier, inc=1, device_id=chip(lax.rem(here + k, nc)), device_id_type=MESH)

    pl.semaphore_signal(barrier, inc=1, device_id=mate, device_id_type=MESH)
    for k in range(1, nx):
        pl.semaphore_signal(barrier, inc=1, device_id={"comp": lax.rem(x + k, nx)}, device_id_type=MESH)

    for k in range(5):
        loads[k].wait()
    mu, var = means[...], varis[...]
    inverse = 1.0 / var
    for h, table in enumerate((mu * inverse, -0.5 * inverse)):
        for part, piece in enumerate(split3(table.T)):
            look[part, h * width : (h + 1) * width, :] = piece
    diagonal = lax.broadcasted_iota(jnp.int32, (kl, kl), 0) == lax.broadcasted_iota(jnp.int32, (kl, kl), 1)

    def column(row):
        return jnp.sum(jnp.where(diagonal, row, 0.0), axis=1, keepdims=True)

    def row_of(col):
        return jnp.sum(jnp.where(diagonal, col, 0.0), axis=0, keepdims=True)

    start_col = column(mass_in[...])
    mcol[...] = jnp.broadcast_to(start_col, mcol.shape)
    offset = jnp.log(start_col) - 0.5 * jnp.sum(jnp.log(var) + mu * mu * inverse, axis=1, keepdims=True)

    steps = 1.0 / plan[...].astype(jnp.float32)
    keep = jnp.ones((1, 1), jnp.float32)
    weight = jnp.zeros(asg.shape, jnp.float32)
    for m in range(plan.shape[1] - 1, -1, -1):
        step = steps[:, m : m + 1]
        chosen = asg[...] == m
        count = jnp.sum(jnp.where(chosen, 1.0, 0.0), axis=1, keepdims=True)
        weight = jnp.where(chosen, step * keep / count, weight)
        keep = keep * (1.0 - step)
    pair_decay[c] = jnp.broadcast_to(keep, (1, kl))
    for b in range(blocks):
        wrow[b] = weight[:, b * BLOCK : (b + 1) * BLOCK]

    def stats_to_peers(b):
        return [
            pltpu.make_async_remote_copy(
                stat.at[b], statin.at[k - 1, b], x_send.at[k - 1, b], x_recv.at[k - 1, b],
                device_id={"comp": lax.rem(x + k, nx)}, device_id_type=MESH,
            )
            for k in range(1, nx)
        ]

    for b in range(blocks):
        loads[5 + b].wait()
    decay_mate = pltpu.make_async_remote_copy(
        pair_decay.at[c], pair_decay.at[c], pair_send.at[4], pair_recv.at[4], device_id=mate, device_id_type=MESH
    )
    early = max(blocks - 1, 1)
    for b in range(blocks):
        p = pts[b]
        first, second = split3(p), split3(p * p)
        for h, f in enumerate((first, second)):
            feat1[h, b] = f[0]
            feat2[h, b] = f[1]
        hi, mid, low = (jnp.concatenate([first[i], second[i]], axis=1) for i in range(3))
        halves = []
        for r in range(2):
            part = slice(r * (BLOCK // 2), (r + 1) * (BLOCK // 2))
            logits = dot_nn(hi[part], look[2]) + dot_nn(low[part], look[0]) + dot_nn(mid[part], look[1])
            logits = logits + dot_nn(hi[part], look[1]) + dot_nn(mid[part], look[0]) + dot_nn(hi[part], look[0])
            halves.append(logits.T + offset)
        logits = jnp.concatenate(halves, axis=1)
        peak = jnp.max(logits, axis=0, keepdims=True)
        e = jnp.exp(logits - peak)
        expo[b] = e
        stat[b, 0:1, :] = peak
        stat[b, 1:2, :] = jnp.sum(e, axis=0, keepdims=True)
        if b == early - 1:
            pl.semaphore_wait(barrier, nc - 1 + 1 + nx - 1)
            decay_mate.start()
            for ready in range(early):
                for copy in stats_to_peers(ready):
                    copy.start()
        if b >= early:
            for copy in stats_to_peers(b):
                copy.start()
    decay_mate.wait()
    decay0, decay1 = pair_decay[0], pair_decay[1]
    decay[...] = decay0 * decay1
    decays[here] = decay0 * decay1
    for q in others:
        pltpu.make_async_remote_copy(
            decay, decays.at[here], decay_send, decay_recv, device_id=chip(q), device_id_type=MESH
        ).start()

    half = kl // 2
    mass = jnp.zeros((kl, 1), jnp.float32)

    def moments(held, h, b):
        return [
            (coarse + dot_nn(wsplit[b, a], feat1[h, b]), fine + dot_nn(wsplit[b, a, 0:half, :], feat2[h, b]))
            for a, (coarse, fine) in enumerate(held)
        ]

    def nothing():
        return [(jnp.zeros((kl, width), jnp.float32), jnp.zeros((half, width), jnp.float32))] * 2

    def summed(held):
        return jnp.concatenate([fine + coarse[half:] + coarse[:half] for coarse, fine in held], axis=0)

    held = nothing()
    for b in range(blocks):
        if b % 2 == 0:
            for copy in stats_to_peers(b) + stats_to_peers(b + 1):
                copy.wait()
        near = stat[b, 0:1, :]
        peaks = [near] + [statin[k, b, 0:1, :] for k in range(nx - 1)]
        sums = [stat[b, 1:2, :]] + [statin[k, b, 1:2, :] for k in range(nx - 1)]
        peak = functools.reduce(jnp.maximum, peaks)
        whole = sum(s * jnp.exp(q - peak) for q, s in zip(peaks, sums))
        scale = jnp.exp(near - peak) / whole * wrow[b]
        w = expo[b] * scale
        mass = mass + jnp.sum(w, axis=1, keepdims=True)
        w1 = w.astype(jnp.bfloat16)
        w2 = (w - w1.astype(jnp.float32)).astype(jnp.bfloat16)
        for a in range(2):
            wsplit[b, a, 0:half, :] = w1[a * half : (a + 1) * half]
            wsplit[b, a, half:kl, :] = w2[a * half : (a + 1) * half]
        held = moments(held, 1 - c, b)
    other[...] = summed(held)
    to_mate = pltpu.make_async_remote_copy(
        other, partner, pair_send.at[0], pair_recv.at[0], device_id=mate, device_id_type=MESH
    )
    to_mate.start()
    pair_mass[c] = row_of(mass)
    mass_mate = pltpu.make_async_remote_copy(
        pair_mass.at[c], pair_mass.at[c], pair_send.at[1], pair_recv.at[1], device_id=mate, device_id_type=MESH
    )
    mass_mate.start()
    held = nothing()
    for b in range(blocks):
        held = moments(held, c, b)
    acc = summed(held)
    mine[...] = acc
    to_mate.wait()

    first_core = c == 0
    one = jnp.ones_like(decay0)
    term[...] = jnp.where(first_core, decay1, one) * acc + jnp.where(first_core, one, decay1) * partner[...]
    for q in others:
        pltpu.make_async_remote_copy(
            term.at[rows(owned(q))], inbuf.at[here], in_send, in_recv, device_id=chip(q), device_id_type=MESH
        ).start()
    mass_mate.wait()
    mass_out[...] = decay1 * pair_mass[0] + pair_mass[1]
    masses[here] = mass_out[...]
    for q in others:
        pltpu.make_async_remote_copy(
            mass_out, masses.at[here], mass_send, mass_recv, device_id=chip(q), device_id_type=MESH
        ).start()
    inbuf[here] = term[rows(own), :]
    mu_own, var_own = means[rows(own), :], varis[rows(own), :]
    s = mcol[rows(own), 0:1] * jnp.where(first_core, mu_own, var_own + mu_own * mu_own)
    drain(decays.at[pl.ds(0, nc - 1)], decay_recv)
    drain(inbuf.at[pl.ds(0, nc - 1)], in_recv)

    def advance(q, s):
        outbuf[q] = s
        return decays[q] * s + inbuf[q]

    s = lax.fori_loop(0, nc, advance, s, unroll=4)
    total[c, rows(own), :] = s

    for k in range(1, nz):
        pltpu.make_async_remote_copy(
            total.at[c, rows(own)], total.at[c, rows(own)], t1_send, t1_recv,
            device_id={"seq_0": lax.rem(z + k, nz)}, device_id_type=MESH,
        ).start()

    for q in others:
        pltpu.make_async_remote_copy(
            outbuf.at[q], carrybuf.at[rows(own)], carry_send, carry_recv, device_id=chip(q), device_id_type=MESH
        ).start()

    carrybuf[rows(own), :] = outbuf[here]

    drain(masses.at[pl.ds(0, nc - 1)], mass_recv)

    def mass_step(q, held):
        ms, entry = held
        entry = jnp.where(q == here, ms, entry)
        return decays[q] * ms + masses[q], entry

    ms, entry_mass = lax.fori_loop(0, nc, mass_step, (mass_in[...], mass_in[...]), unroll=4)

    def lines(row):
        return pl.ds(pl.multiple_of(row * nz * share, nz * share), nz * share)

    def line_to_mate(row):
        return pltpu.make_async_remote_copy(
            total.at[c, lines(row)], total.at[c, lines(row)], pair_send.at[2], pair_recv.at[2],
            device_id=mate, device_id_type=MESH,
        )

    drain(total.at[0, pl.ds(0, (nz - 1) * share)], t1_recv)
    for k in range(1, ny):
        pltpu.make_async_remote_copy(
            total.at[c, lines(y)], total.at[c, lines(y)], t2_send, t2_recv.at[k - 1],
            device_id={"seq_1": lax.rem(y + k, ny)}, device_id_type=MESH,
        ).start()
    line_to_mate(y).start()

    drain(carrybuf.at[pl.ds(0, (nc - 1) * share)], carry_recv)
    from_own, from_mate = mine[...], partner[...]
    state0 = decay0 * carrybuf[...] + jnp.where(first_core, from_own, from_mate)
    state1 = decay1 * state0 + jnp.where(first_core, from_mate, from_own)
    stateout[...] = jnp.where(first_core, state1, state0)
    state_mate = pltpu.make_async_remote_copy(
        stateout, state.at[c], pair_send.at[3], pair_recv.at[3], device_id=mate, device_id_type=MESH
    )
    state_mate.start()
    state[c] = jnp.where(first_core, state0, state1)
    for k in range(1, ny):
        drain(total.at[0, pl.ds(0, nz * share)], t2_recv.at[k - 1])
        line_to_mate(lax.rem(y - k + ny, ny)).start()
    mass0 = decay0 * entry_mass + pair_mass[0]
    mass1 = decay1 * mass0 + pair_mass[1]
    mass_row = jnp.where(first_core, mass0, mass1)
    dlog[...] = jnp.log(mass_row)
    flog[...] = jnp.log(ms)
    inv_dev, inv_final = 1.0 / column(mass_row), 1.0 / column(ms)

    state_mate.wait()
    centers = state[0] * inv_dev
    dmean[...] = centers
    dvar[...] = state[1] * inv_dev - centers * centers + VAR_PRIOR
    drain(total.at[0], pair_recv.at[2])
    centers = total[0] * inv_final
    fmean[...] = centers
    fvar[...] = total[1] * inv_final - centers * centers + VAR_PRIOR

    drain(total.at[0], pair_send.at[2])
    drain(masses.at[pl.ds(0, nc - 1)], mass_send)
    drain(decays.at[pl.ds(0, nc - 1)], decay_send)
    drain(inbuf.at[pl.ds(0, nc - 1)], in_send)
    drain(carrybuf.at[pl.ds(0, (nc - 1) * share)], carry_send)
    drain(total.at[0, pl.ds(0, (nz - 1) * share)], t1_send)
    drain(total.at[0, pl.ds(0, (ny - 1) * nz * share)], t2_send)


def deliver(*refs):
    copies = [pltpu.make_async_copy(refs[k], refs[6 + k], refs[12].at[k]) for k in range(6)]
    for copy in copies:
        copy.start()
    for copy in copies:
        copy.wait()


def local(nz, ny, nx, points, assign, plan, init_mass, init_means, init_vars):
    kl, width = init_means.shape
    count = points.shape[0]
    nc, blocks = nz * ny, count // BLOCK
    share = kl // nc
    f32, bf16 = jnp.float32, jnp.bfloat16
    vmem, hbm, dma = pltpu.VMEM, pltpu.HBM, pltpu.SemaphoreType.DMA
    row, table = jax.ShapeDtypeStruct((1, kl), f32), jax.ShapeDtypeStruct((kl, width), f32)
    far = functools.partial(pltpu.with_memory_space_constraint, memory_space=hbm)
    outs = pl.pallas_call(
        functools.partial(kernel, nz, ny, nx),
        out_shape=(row, table, table, row, table, table),
        in_specs=[pl.BlockSpec(memory_space=hbm)] * 6,
        out_specs=[pl.BlockSpec(memory_space=vmem)] * 6,
        scratch_shapes=[
            vmem((blocks, BLOCK, width), f32),
            vmem((kl, width), f32),
            vmem((kl, width), f32),
            vmem((1, count), jnp.int32),
            vmem(plan.shape, jnp.int32),
            vmem((1, kl), f32),
            dma((5 + blocks,)),
            vmem((3, 2 * width, kl), bf16),
            vmem((2, blocks, BLOCK, width), bf16),
            vmem((2, blocks, BLOCK, width), bf16),
            vmem((blocks, kl, BLOCK), f32),
            vmem((blocks, 2, kl, BLOCK), bf16),
            vmem((blocks, 1, BLOCK), f32),
            vmem((kl, 128), f32),
            vmem((blocks, 2, BLOCK), f32),
            vmem((nx - 1, blocks, 2, BLOCK), f32),
            vmem((kl, width), f32),
            vmem((kl, width), f32),
            vmem((kl, width), f32),
            vmem((2, 1, kl), f32),
            vmem((2, 1, kl), f32),
            vmem((1, kl), f32),
            vmem((nc, 1, kl), f32),
            vmem((1, kl), f32),
            vmem((nc, 1, kl), f32),
            vmem((kl, width), f32),
            vmem((nc, share, width), f32),
            vmem((nc, share, width), f32),
            vmem((kl, width), f32),
            vmem((2, kl, width), f32),
            vmem((2, kl, width), f32),
            vmem((kl, width), f32),
            dma((nx - 1, blocks)), dma((nx - 1, blocks)),
            dma((5,)), dma((5,)),
            dma, dma, dma, dma, dma, dma, dma, dma, dma, dma, dma, dma((ny - 1,)),
        ],
        compiler_params=pltpu.CompilerParams(collective_id=0, has_side_effects=True, vmem_limit_bytes=32 * 2**20),
    )(*(far(a) for a in (points, assign, plan, init_mass.reshape(1, kl), init_means, init_vars)))
    outs = pl.pallas_call(
        deliver,
        out_shape=tuple(jax.ShapeDtypeStruct(o.shape, f32) for o in outs),
        in_specs=[pl.BlockSpec(memory_space=vmem)] * 6,
        out_specs=[pl.BlockSpec(memory_space=hbm)] * 6,
        scratch_shapes=[dma((6,))],
        compiler_params=pltpu.CompilerParams(vmem_limit_bytes=2 * 2**20),
    )(*outs)
    return tuple(o.reshape(1, kl) if o.shape[0] == 1 else o[None] for o in outs)


def solution(mesh):
    nz, ny, nx = 8, 4, mesh.shape["comp"]
    split = Mesh(mesh.devices.reshape(nz, ny, 2, nx), (*SEQ, "comp"))
    return jax.shard_map(
        functools.partial(local, nz, ny, nx),
        mesh=split,
        in_specs=(P(SEQ, None), P(SEQ, None), P(SEQ, None), P("comp"), P("comp", None), P("comp", None)),
        out_specs=(
            P(SEQ, "comp"), P(SEQ, "comp", None), P(SEQ, "comp", None),
            P(SEQ, "comp"), P(SEQ, "comp", None), P(SEQ, "comp", None),
        ),
        check_vma=False,
    )
```

time: 60.4 us -> 44.6 us (0.74)
  local copies, waits for them, and re-layouts: 9.13 us -> 0 us
  Pallas kernels: 50.4 us -> 43.9 us
    unnamed x6 -> x0, local copies, waits for them, and re-layouts: 9.13 us -> none
    pallas_call x1, Pallas kernels: 50.4 us -> 42.8 us  [local(): pl.pallas_call(functools.partial(kernel, nz, ny, nx), out_shape=(row, tab...]
    pallas_call x0 -> x1, Pallas kernels: none -> 1.03 us  [local(): pl.pallas_call(deliver, out_shape=tuple((jax.ShapeDtypeStruct(o.shape, f3...]
where the time goes in v2:
time: 44.6 us; the launch traced here: 44.5 us
  Pallas kernels  43.9 us (98%)
  between operations  0.64 us (1%)
    pallas_call x1, Pallas kernels, local(): pl.pallas_call(functools.partial(kernel, nz, ny, nx), out_shape=(row, tab...  42.8 us
    pallas_call x1, Pallas kernels, local(): pl.pallas_call(deliver, out_shape=tuple((jax.ShapeDtypeStruct(o.shape, f3...  1.03 us

profile of v2, /device:TPU:1, one launch (start us, length us, event | category | flops | bytes accessed | tf_op | source)
XLA Modules:
  0.0 44.5 jit_solution(18074865813429758773)
XLA Ops:
  0.6 42.8 %shard_map.109 = (f32[1,256]{1,0:T(1,128)S(1)}, f32[256,256]{1,0:T(8,128)S(1)}, f32[256,256]{1,0:T(8,128)S(1)}, f32[1,256]{1,0:T(1,128)S(1)}, f32[256,256]{1,0:T(8,128)S(1)}, /*index=5*/f32[256,256]{1,0:T(8,128)S(1)}) custom-call(f32[2048,256]{1,0:T(8,128)} %pts_in.1, s32[1,2048]{1,0:T(1,128)} %asg_in.1, s32[1,4]{1,0:T(1,128)} %plan_in.1, f32[1,256]{1,0:T(1,128)} %bitcast.5, ...), custom_call_target="tpu_custom_call" | custom-call | tf_op jit(solution)/shard_map/pallas_call | solution.py:352
  43.5 1.0 %shard_map.110 = (f32[1,256]{1,0:T(1,128)}, f32[256,256]{1,0:T(8,128)}, f32[256,256]{1,0:T(8,128)}, f32[1,256]{1,0:T(1,128)}, f32[256,256]{1,0:T(8,128)}, /*index=5*/f32[256,256]{1,0:T(8,128)}) custom-call(f32[1,256]{1,0:T(1,128)S(1)} %get-tuple-element.18.refs_0_, f32[256,256]{1,0:T(8,128)S(1)} %get-tuple-element.19.refs_1_, ...), custom_call_target="tpu_custom_call" | custom-call | tf_op jit(solution)/shard_map/pallas_call | solution.py:396

commit v3 on v2

--- a/solution.py
+++ b/solution.py
@@ -12,6 +12,7 @@
 MESH = pl.DeviceIdType.MESH
 VAR_PRIOR = 0.01
 BLOCK = 512
+PARTS = 2
 
 
 def split3(a):
@@ -40,10 +41,11 @@
     dlog, dmean, dvar, flog, fmean, fvar,
     pts, means, varis, asg, plan, mass_in, load,
     look, feat1, feat2, expo, wsplit, wrow, mcol,
-    stat, statin, mine, other, partner, pair_decay, pair_mass, decay, decays, mass_out, masses,
-    term, inbuf, outbuf, carrybuf, total, state, stateout,
-    x_send, x_recv, pair_send, pair_recv, in_send, in_recv, mass_send, mass_recv, decay_send, decay_recv,
-    carry_send, carry_recv, t1_send, t1_recv, t2_send, t2_recv,
+    stat, statin, mine, other, partner, pair_decay, pair_mass, decay_y, decay_z, mass_y, mass_z,
+    term, terms, before, plane, planes, entry, entries, lines, linein, state, stateout, mystate, total,
+    inv_dev, inv_final,
+    x_send, x_recv, pair_send, pair_recv, term_send, term_recv, plane_send, plane_recv, entry_send, entry_recv,
+    line_send, line_recv, decay_send, decay_recv, mass_send, mass_recv, chunk_send, chunk_recv,
 ):
     loads = [
         pltpu.make_async_copy(means_in, means, load.at[0]),
@@ -61,34 +63,44 @@
     kl, width = means.shape
     share = kl // nc
     blocks = pts.shape[0]
-    here = z * ny + y
-    own = y * nz + z
-
-    def owned(q):
-        return lax.rem(q, ny) * nz + q // ny
-
-    def chip(q):
-        return {"seq_0": q // ny, "seq_1": lax.rem(q, ny)}
-
-    def rows(o):
-        return pl.ds(pl.multiple_of(o * share, share), share)
-
+    band = kl // ny
     mate = {"seq_2": 1 - c}
 
-    def away(offset, size):
-        return min(offset, size - offset)
-
-    offsets = [(dz, dy) for dz in range(nz) for dy in range(ny) if dz or dy]
-
-    offsets.sort(key=lambda d: away(d[0], nz) + away(d[1], ny))
-    others = [lax.rem(z + dz, nz) * ny + lax.rem(y + dy, ny) for dz, dy in offsets]
+    def spread(size):
+        near = sorted(range(1, size), key=lambda k: min(k, size - k))
+        return [near[-1 - k // 2] if k % 2 == 0 else near[k // 2] for k in range(len(near))]
+
+    def along_y(k):
+        return lax.rem(y + k, ny)
+
+    def along_z(k):
+        return lax.rem(z + k, nz)
+
+    def band_rows(q):
+        return pl.ds(pl.multiple_of(q * band, band), band)
+
+    def rows(q):
+        return pl.ds(pl.multiple_of(q * share, share), share)
+
+    def to_y(k, src, dst, send, recv):
+        return pltpu.make_async_remote_copy(
+            src, dst, send, recv, device_id={"seq_1": along_y(k)}, device_id_type=MESH
+        )
+
+    def to_z(k, src, dst, send, recv):
+        return pltpu.make_async_remote_copy(
+            src, dst, send, recv, device_id={"seq_0": along_z(k)}, device_id_type=MESH
+        )
+
+    def to_mate(src, dst, send, recv):
+        return pltpu.make_async_remote_copy(src, dst, send, recv, device_id=mate, device_id_type=MESH)
 
     barrier = pltpu.get_barrier_semaphore()
 
-    @pl.loop(1, nc)
-    def _(k):
-        pl.semaphore_signal(barrier, inc=1, device_id=chip(lax.rem(here + k, nc)), device_id_type=MESH)
-
+    for k in range(1, nz):
+        pl.semaphore_signal(barrier, inc=1, device_id={"seq_0": along_z(k)}, device_id_type=MESH)
+    for k in range(1, ny):
+        pl.semaphore_signal(barrier, inc=1, device_id={"seq_1": along_y(k)}, device_id_type=MESH)
     pl.semaphore_signal(barrier, inc=1, device_id=mate, device_id_type=MESH)
     for k in range(1, nx):
         pl.semaphore_signal(barrier, inc=1, device_id={"comp": lax.rem(x + k, nx)}, device_id_type=MESH)
@@ -136,9 +148,7 @@
 
     for b in range(blocks):
         loads[5 + b].wait()
-    decay_mate = pltpu.make_async_remote_copy(
-        pair_decay.at[c], pair_decay.at[c], pair_send.at[4], pair_recv.at[4], device_id=mate, device_id_type=MESH
-    )
+    decay_mate = to_mate(pair_decay.at[c], pair_decay.at[c], pair_send.at[0], pair_recv.at[0])
     early = max(blocks - 1, 1)
     for b in range(blocks):
         p = pts[b]
@@ -160,7 +170,7 @@
         stat[b, 0:1, :] = peak
         stat[b, 1:2, :] = jnp.sum(e, axis=0, keepdims=True)
         if b == early - 1:
-            pl.semaphore_wait(barrier, nc - 1 + 1 + nx - 1)
+            pl.semaphore_wait(barrier, nz - 1 + ny - 1 + 1 + nx - 1)
             decay_mate.start()
             for ready in range(early):
                 for copy in stats_to_peers(ready):
@@ -170,12 +180,9 @@
                 copy.start()
     decay_mate.wait()
     decay0, decay1 = pair_decay[0], pair_decay[1]
-    decay[...] = decay0 * decay1
-    decays[here] = decay0 * decay1
-    for q in others:
-        pltpu.make_async_remote_copy(
-            decay, decays.at[here], decay_send, decay_recv, device_id=chip(q), device_id_type=MESH
-        ).start()
+    decay_y[y] = decay0 * decay1
+    for k in spread(ny):
+        to_y(k, decay_y.at[y], decay_y.at[y], decay_send.at[0], decay_recv.at[0]).start()
 
     half = kl // 2
     mass = jnp.zeros((kl, 1), jnp.float32)
@@ -212,124 +219,153 @@
             wsplit[b, a, half:kl, :] = w2[a * half : (a + 1) * half]
         held = moments(held, 1 - c, b)
     other[...] = summed(held)
-    to_mate = pltpu.make_async_remote_copy(
-        other, partner, pair_send.at[0], pair_recv.at[0], device_id=mate, device_id_type=MESH
-    )
-    to_mate.start()
+    other_mate = to_mate(other, partner, pair_send.at[1], pair_recv.at[1])
+    other_mate.start()
     pair_mass[c] = row_of(mass)
-    mass_mate = pltpu.make_async_remote_copy(
-        pair_mass.at[c], pair_mass.at[c], pair_send.at[1], pair_recv.at[1], device_id=mate, device_id_type=MESH
-    )
+    mass_mate = to_mate(pair_mass.at[c], pair_mass.at[c], pair_send.at[2], pair_recv.at[2])
     mass_mate.start()
+    drain(decay_y.at[pl.ds(0, ny - 1)], decay_recv.at[0])
+    decay_z[z] = decay_y[...]
+    for k in spread(nz):
+        to_z(k, decay_y, decay_z.at[z], decay_send.at[1], decay_recv.at[1]).start()
     held = nothing()
     for b in range(blocks):
         held = moments(held, c, b)
     acc = summed(held)
     mine[...] = acc
-    to_mate.wait()
+    other_mate.wait()
 
     first_core = c == 0
+    lanes = width // PARTS
+
+    def cut(h):
+        return slice(h * lanes, (h + 1) * lanes)
+
+    def thin(row):
+        return row[:, 0:lanes]
+
     one = jnp.ones_like(decay0)
-    term[...] = jnp.where(first_core, decay1, one) * acc + jnp.where(first_core, one, decay1) * partner[...]
-    for q in others:
-        pltpu.make_async_remote_copy(
-            term.at[rows(owned(q))], inbuf.at[here], in_send, in_recv, device_id=chip(q), device_id_type=MESH
-        ).start()
+    combined = jnp.where(first_core, decay1, one) * acc + jnp.where(first_core, one, decay1) * partner[...]
+    for h in range(PARTS):
+        term[h] = combined[:, cut(h)]
+        for k in spread(ny):
+            to_y(k, term.at[h, band_rows(along_y(k))], terms.at[h, y], term_send.at[h], term_recv.at[h]).start()
+        terms[h, y] = term[h, band_rows(y), :]
     mass_mate.wait()
-    mass_out[...] = decay1 * pair_mass[0] + pair_mass[1]
-    masses[here] = mass_out[...]
-    for q in others:
-        pltpu.make_async_remote_copy(
-            mass_out, masses.at[here], mass_send, mass_recv, device_id=chip(q), device_id_type=MESH
-        ).start()
-    inbuf[here] = term[rows(own), :]
-    mu_own, var_own = means[rows(own), :], varis[rows(own), :]
-    s = mcol[rows(own), 0:1] * jnp.where(first_core, mu_own, var_own + mu_own * mu_own)
-    drain(decays.at[pl.ds(0, nc - 1)], decay_recv)
-    drain(inbuf.at[pl.ds(0, nc - 1)], in_recv)
-
-    def advance(q, s):
-        outbuf[q] = s
-        return decays[q] * s + inbuf[q]
-
-    s = lax.fori_loop(0, nc, advance, s, unroll=4)
-    total[c, rows(own), :] = s
-
-    for k in range(1, nz):
-        pltpu.make_async_remote_copy(
-            total.at[c, rows(own)], total.at[c, rows(own)], t1_send, t1_recv,
-            device_id={"seq_0": lax.rem(z + k, nz)}, device_id_type=MESH,
-        ).start()
-
-    for q in others:
-        pltpu.make_async_remote_copy(
-            outbuf.at[q], carrybuf.at[rows(own)], carry_send, carry_recv, device_id=chip(q), device_id_type=MESH
-        ).start()
-
-    carrybuf[rows(own), :] = outbuf[here]
-
-    drain(masses.at[pl.ds(0, nc - 1)], mass_recv)
-
-    def mass_step(q, held):
-        ms, entry = held
-        entry = jnp.where(q == here, ms, entry)
-        return decays[q] * ms + masses[q], entry
-
-    ms, entry_mass = lax.fori_loop(0, nc, mass_step, (mass_in[...], mass_in[...]), unroll=4)
-
-    def lines(row):
-        return pl.ds(pl.multiple_of(row * nz * share, nz * share), nz * share)
-
-    def line_to_mate(row):
-        return pltpu.make_async_remote_copy(
-            total.at[c, lines(row)], total.at[c, lines(row)], pair_send.at[2], pair_recv.at[2],
-            device_id=mate, device_id_type=MESH,
-        )
-
-    drain(total.at[0, pl.ds(0, (nz - 1) * share)], t1_recv)
-    for k in range(1, ny):
-        pltpu.make_async_remote_copy(
-            total.at[c, lines(y)], total.at[c, lines(y)], t2_send, t2_recv.at[k - 1],
-            device_id={"seq_1": lax.rem(y + k, ny)}, device_id_type=MESH,
-        ).start()
-    line_to_mate(y).start()
-
-    drain(carrybuf.at[pl.ds(0, (nc - 1) * share)], carry_recv)
-    from_own, from_mate = mine[...], partner[...]
-    state0 = decay0 * carrybuf[...] + jnp.where(first_core, from_own, from_mate)
-    state1 = decay1 * state0 + jnp.where(first_core, from_mate, from_own)
-    stateout[...] = jnp.where(first_core, state1, state0)
-    state_mate = pltpu.make_async_remote_copy(
-        stateout, state.at[c], pair_send.at[3], pair_recv.at[3], device_id=mate, device_id_type=MESH
-    )
-    state_mate.start()
-    state[c] = jnp.where(first_core, state0, state1)
-    for k in range(1, ny):
-        drain(total.at[0, pl.ds(0, nz * share)], t2_recv.at[k - 1])
-        line_to_mate(lax.rem(y - k + ny, ny)).start()
+    mass_y[y] = decay1 * pair_mass[0] + pair_mass[1]
+    for k in spread(ny):
+        to_y(k, mass_y.at[y], mass_y.at[y], mass_send.at[0], mass_recv.at[0]).start()
+    mu_own, var_own = means[rows(y * nz + z), :], varis[rows(y * nz + z), :]
+    start = mcol[rows(y * nz + z), 0:1] * jnp.where(first_core, mu_own, var_own + mu_own * mu_own)
+
+    for h in range(PARTS):
+        drain(terms.at[h, pl.ds(0, ny - 1)], term_recv.at[h])
+        held = terms[h, 0]
+        for q in range(1, ny):
+            before[h, q] = held
+            held = thin(decay_y[q]) * held + terms[h, q]
+        plane[h] = held
+        for k in spread(nz):
+            to_z(k, plane.at[h, rows(along_z(k))], planes.at[h, z], plane_send.at[h], plane_recv.at[h]).start()
+        planes[h, z] = plane[h, rows(z), :]
+    drain(mass_y.at[pl.ds(0, ny - 1)], mass_recv.at[0])
+    mass_z[z] = mass_y[...]
+    for k in spread(nz):
+        to_z(k, mass_y, mass_z.at[z], mass_send.at[1], mass_recv.at[1]).start()
+    drain(decay_z.at[pl.ds(0, nz - 1)], decay_recv.at[1])
+    plane_decay = [thin(functools.reduce(jnp.multiply, [decay_z[q, r] for r in range(ny)])) for q in range(nz)]
+
+    for h in range(PARTS):
+        drain(planes.at[h, pl.ds(0, nz - 1)], plane_recv.at[h])
+        s = start[:, cut(h)]
+        for q in range(nz):
+            entry[h, q, 0] = s
+            s = plane_decay[q] * s + planes[h, q]
+        for q in range(nz):
+            entry[h, q, 1] = s
+        for k in spread(nz):
+            to_z(k, entry.at[h, along_z(k)], entries.at[h, z], entry_send.at[h], entry_recv.at[h]).start()
+        entries[h, z] = entry[h, z]
+
+    drain(mass_z.at[pl.ds(0, nz - 1)], mass_recv.at[1])
+    ms = mass_in[...]
+    entry_mass = ms
+    for q in range(nz):
+        for r in range(ny):
+            entry_mass = jnp.where(jnp.logical_and(q == z, r == y), ms, entry_mass)
+            ms = decay_z[q, r] * ms + mass_z[q, r]
     mass0 = decay0 * entry_mass + pair_mass[0]
     mass1 = decay1 * mass0 + pair_mass[1]
     mass_row = jnp.where(first_core, mass0, mass1)
     dlog[...] = jnp.log(mass_row)
     flog[...] = jnp.log(ms)
-    inv_dev, inv_final = 1.0 / column(mass_row), 1.0 / column(ms)
-
-    state_mate.wait()
-    centers = state[0] * inv_dev
-    dmean[...] = centers
-    dvar[...] = state[1] * inv_dev - centers * centers + VAR_PRIOR
-    drain(total.at[0], pair_recv.at[2])
-    centers = total[0] * inv_final
-    fmean[...] = centers
-    fvar[...] = total[1] * inv_final - centers * centers + VAR_PRIOR
-
-    drain(total.at[0], pair_send.at[2])
-    drain(masses.at[pl.ds(0, nc - 1)], mass_send)
-    drain(decays.at[pl.ds(0, nc - 1)], decay_send)
-    drain(inbuf.at[pl.ds(0, nc - 1)], in_send)
-    drain(carrybuf.at[pl.ds(0, (nc - 1) * share)], carry_send)
-    drain(total.at[0, pl.ds(0, (nz - 1) * share)], t1_send)
-    drain(total.at[0, pl.ds(0, (ny - 1) * nz * share)], t2_send)
+    inv_dev[...] = jnp.broadcast_to(1.0 / column(mass_row), inv_dev.shape)
+    inv_final[...] = jnp.broadcast_to(1.0 / column(ms), inv_final.shape)
+
+    for h in range(PARTS):
+        drain(entries.at[h, pl.ds(0, nz - 1)], entry_recv.at[h])
+        carry, whole = entries[h, :, 0].reshape(band, lanes), entries[h, :, 1].reshape(band, lanes)
+        ahead = thin(one)
+        for q in range(ny):
+            lines[h, q, 0] = ahead * carry + before[h, q] if q else carry
+            lines[h, q, 1] = whole
+            ahead = ahead * thin(decay_y[q])
+        for k in spread(ny):
+            to_y(k, lines.at[h, along_y(k)], linein.at[h, y], line_send.at[h], line_recv.at[h, k - 1]).start()
+        linein[h, y] = lines[h, y]
+
+    arrivals = [0] + sorted(range(1, ny), key=lambda k: min(k, ny - k))
+    order = [(h, k) for h in range(PARTS) for k in arrivals]
+
+    def from_band(k):
+        return lax.rem(y - k + ny, ny)
+
+    def band_to_mate(at, h, k):
+        source = from_band(k)
+        return (
+            to_mate(linein.at[h, source, 1], total.at[h, source], chunk_send.at[2 * at], chunk_recv.at[2 * at]),
+            to_mate(stateout.at[h, source], state.at[h, source], chunk_send.at[2 * at + 1], chunk_recv.at[2 * at + 1]),
+        )
+
+    for at, (h, k) in enumerate(order):
+        source = from_band(k)
+        if k:
+            drain(linein.at[h, 0], line_recv.at[h, k - 1])
+        total_mate, state_mate = band_to_mate(at, h, k)
+        total_mate.start()
+        from_own, from_mate = mine[band_rows(source), cut(h)], partner[band_rows(source), cut(h)]
+        state0 = thin(decay0) * linein[h, source, 0] + jnp.where(first_core, from_own, from_mate)
+        state1 = thin(decay1) * state0 + jnp.where(first_core, from_mate, from_own)
+        stateout[h, source] = jnp.where(first_core, state1, state0)
+        state_mate.start()
+        mystate[h, source] = jnp.where(first_core, state0, state1)
+
+    for at, (h, k) in enumerate(order):
+        source = from_band(k)
+        part = band_rows(source)
+        total_mate, state_mate = band_to_mate(at, h, k)
+        total_mate.wait()
+        near, far = linein[h, source, 1], total[h, source]
+        scale = inv_final[part, 0:1]
+        centers = jnp.where(first_core, near, far) * scale
+        fmean[part, cut(h)] = centers
+        fvar[part, cut(h)] = jnp.where(first_core, far, near) * scale - centers * centers + VAR_PRIOR
+        state_mate.wait()
+        near, far = mystate[h, source], state[h, source]
+        scale = inv_dev[part, 0:1]
+        centers = jnp.where(first_core, near, far) * scale
+        dmean[part, cut(h)] = centers
+        dvar[part, cut(h)] = jnp.where(first_core, far, near) * scale - centers * centers + VAR_PRIOR
+
+    for h in range(PARTS):
+        drain(terms.at[h, pl.ds(0, ny - 1)], term_send.at[h])
+        drain(planes.at[h, pl.ds(0, nz - 1)], plane_send.at[h])
+        drain(entries.at[h, pl.ds(0, nz - 1)], entry_send.at[h])
+        drain(linein.at[h, pl.ds(0, ny - 1)], line_send.at[h])
+    drain(decay_y.at[pl.ds(0, ny - 1)], decay_send.at[0])
+    drain(decay_z.at[pl.ds(0, nz - 1)], decay_send.at[1])
+    drain(mass_y.at[pl.ds(0, ny - 1)], mass_send.at[0])
+    drain(mass_z.at[pl.ds(0, nz - 1)], mass_send.at[1])
 
 
 def deliver(*refs):
@@ -344,7 +380,7 @@
     kl, width = init_means.shape
     count = points.shape[0]
     nc, blocks = nz * ny, count // BLOCK
-    share = kl // nc
+    share, band, lanes = kl // nc, kl // ny, width // PARTS
     f32, bf16 = jnp.float32, jnp.bfloat16
     vmem, hbm, dma = pltpu.VMEM, pltpu.HBM, pltpu.SemaphoreType.DMA
     row, table = jax.ShapeDtypeStruct((1, kl), f32), jax.ShapeDtypeStruct((kl, width), f32)
@@ -376,20 +412,30 @@
             vmem((kl, width), f32),
             vmem((2, 1, kl), f32),
             vmem((2, 1, kl), f32),
-            vmem((1, kl), f32),
-            vmem((nc, 1, kl), f32),
-            vmem((1, kl), f32),
-            vmem((nc, 1, kl), f32),
-            vmem((kl, width), f32),
-            vmem((nc, share, width), f32),
-            vmem((nc, share, width), f32),
-            vmem((kl, width), f32),
-            vmem((2, kl, width), f32),
-            vmem((2, kl, width), f32),
-            vmem((kl, width), f32),
+            vmem((ny, 1, kl), f32),
+            vmem((nz, ny, 1, kl), f32),
+            vmem((ny, 1, kl), f32),
+            vmem((nz, ny, 1, kl), f32),
+            vmem((PARTS, kl, lanes), f32),
+            vmem((PARTS, ny, band, lanes), f32),
+            vmem((PARTS, ny, band, lanes), f32),
+            vmem((PARTS, band, lanes), f32),
+            vmem((PARTS, nz, share, lanes), f32),
+            vmem((PARTS, nz, 2, share, lanes), f32),
+            vmem((PARTS, nz, 2, share, lanes), f32),
+            vmem((PARTS, ny, 2, band, lanes), f32),
+            vmem((PARTS, ny, 2, band, lanes), f32),
+            vmem((PARTS, ny, band, lanes), f32),
+            vmem((PARTS, ny, band, lanes), f32),
+            vmem((PARTS, ny, band, lanes), f32),
+            vmem((PARTS, ny, band, lanes), f32),
+            vmem((kl, 128), f32),
+            vmem((kl, 128), f32),
             dma((nx - 1, blocks)), dma((nx - 1, blocks)),
-            dma((5,)), dma((5,)),
-            dma, dma, dma, dma, dma, dma, dma, dma, dma, dma, dma, dma((ny - 1,)),
+            dma((3,)), dma((3,)),
+            dma((PARTS,)), dma((PARTS,)), dma((PARTS,)), dma((PARTS,)), dma((PARTS,)), dma((PARTS,)),
+            dma((PARTS,)), dma((PARTS, ny - 1)), dma((2,)), dma((2,)), dma((2,)), dma((2,)),
+            dma((2 * PARTS * ny,)), dma((2 * PARTS * ny,)),
         ],
         compiler_params=pltpu.CompilerParams(collective_id=0, has_side_effects=True, vmem_limit_bytes=32 * 2**20),
     )(*(far(a) for a in (points, assign, plan, init_mass.reshape(1, kl), init_means, init_vars)))

time: 44.6 us -> 41.7 us (0.935)
  Pallas kernels: 43.9 us -> 40.9 us
    pallas_call x1, Pallas kernels: 42.8 us -> 39.9 us  [local(): pl.pallas_call(functools.partial(kernel, nz, ny, nx), out_shape=(row, tab...]
where the time goes in v3:
time: 41.7 us; the launch traced here: 41.6 us
  Pallas kernels  40.9 us (98%)
  between operations  0.64 us (2%)
    pallas_call x1, Pallas kernels, local(): pl.pallas_call(functools.partial(kernel, nz, ny, nx), out_shape=(row, tab...  39.9 us
    pallas_call x1, Pallas kernels, local(): pl.pallas_call(deliver, out_shape=tuple((jax.ShapeDtypeStruct(o.shape, f3...  1.03 us

profile of v3, /device:TPU:1, one launch (start us, length us, event | category | flops | bytes accessed | tf_op | source)
XLA Modules:
  0.0 41.6 jit_solution(15933601299815505151)
XLA Ops:
  0.6 39.9 %shard_map.109 = (f32[1,256]{1,0:T(1,128)S(1)}, f32[256,256]{1,0:T(8,128)S(1)}, f32[256,256]{1,0:T(8,128)S(1)}, f32[1,256]{1,0:T(1,128)S(1)}, f32[256,256]{1,0:T(8,128)S(1)}, /*index=5*/f32[256,256]{1,0:T(8,128)S(1)}) custom-call(f32[2048,256]{1,0:T(8,128)} %pts_in.1, s32[1,2048]{1,0:T(1,128)} %asg_in.1, s32[1,4]{1,0:T(1,128)} %plan_in.1, f32[1,256]{1,0:T(1,128)} %bitcast.5, ...), custom_call_target="tpu_custom_call" | custom-call | tf_op jit(solution)/shard_map/pallas_call | solution.py:388
  40.6 1.0 %shard_map.110 = (f32[1,256]{1,0:T(1,128)}, f32[256,256]{1,0:T(8,128)}, f32[256,256]{1,0:T(8,128)}, f32[1,256]{1,0:T(1,128)}, f32[256,256]{1,0:T(8,128)}, /*index=5*/f32[256,256]{1,0:T(8,128)}) custom-call(f32[1,256]{1,0:T(1,128)S(1)} %get-tuple-element.18.refs_0_, f32[256,256]{1,0:T(8,128)S(1)} %get-tuple-element.19.refs_1_, ...), custom_call_target="tpu_custom_call" | custom-call | tf_op jit(solution)/shard_map/pallas_call | solution.py:442
